TPU v7x, 32 devices: a whole 2x2x4 slice. The times are simulated.
32 devices in a mesh: row: 8 (over z, x), col: 4 (over y, core).
Axes of the slice: x: 2, y: 2, z: 4, core: 2. Of those that a mesh axis runs over, the one named last changes fastest.
Arguments:
- factor: float32 [9, 1024, 3, 512], P(None, 'row', None, 'col'), may hold values from -2 to 2.5, as said below
- adjoint: float32 [9, 1024, 3, 512], P(None, 'row', None, 'col'), may hold values from -6 to 6
Outputs:
- kernel_adjoint: float32 [9, 1024, 3, 512], P(None, 'row', None, 'col')
Inputs may be any that keep to these rules, and one draw needn't show every extreme that they name: `factor`: zero where the column minus 512 exceeds the row; the diagonal entries of the two 512-square diagonal blocks lie between 1 and 2.5.
All inputs are finite; a program needn't handle non-finite values.
Results may differ from a plain program's by a relative error of at most 0.0001.
Values sent between devices are 32-bit elements; how exact they have to be, the bound alone decides.
A program may use at most 64 MiB of HBM per device.

v0:
```python
import jax
import jax.numpy as jnp
from jax import lax
from jax.sharding import PartitionSpec as P

NB = 512


def exact_dot(first, second):
    return jnp.dot(
        first, second, precision=lax.Precision.HIGHEST, preferred_element_type=jnp.float32
    )


def lower_half(matrix):
    return jnp.tril(matrix) - 0.5 * jnp.diag(jnp.diag(matrix))


def local(factor, adjoint):
    row_cycles, tile_rows, col_cycles, tile_cols = factor.shape
    col_devices = lax.axis_size("col")
    row_devices = lax.axis_size("row")
    row_span = tile_rows * row_devices
    col_span = tile_cols * col_devices
    row_index = lax.axis_index("row")
    col_index = lax.axis_index("col")
    local_rows = row_cycles * tile_rows
    local_cols = col_cycles * tile_cols
    left_cols = col_cycles * col_span - 2 * NB
    panel_cycles = 2 * NB // col_span
    row_blocks = 2 * NB // row_span
    owned_rows = row_blocks * tile_rows
    owned_cols = panel_cycles * tile_cols
    split_col = local_cols - owned_cols
    row_steps = jnp.arange(local_rows, dtype=jnp.int32)
    col_steps = jnp.arange(local_cols, dtype=jnp.int32)
    global_rows = row_steps // tile_rows * row_span + row_index * tile_rows + row_steps % tile_rows
    global_cols = col_steps // tile_cols * col_span + col_index * tile_cols + col_steps % tile_cols
    factor_flat = factor.reshape(local_rows, local_cols)
    working = jnp.where(
        global_cols[None, :] - left_cols > global_rows[:, None],
        0.0,
        adjoint.reshape(local_rows, local_cols),
    )
    factor_local = factor_flat[:, split_col:].reshape(local_rows, panel_cycles, tile_cols)
    factor_panels = lax.all_gather(factor_local, "col", axis=2, tiled=True).reshape(
        local_rows, 2 * NB
    )
    factor_tops = factor_flat[:owned_rows].reshape(row_blocks, tile_rows, local_cols)
    diag_part = factor_panels[:owned_rows].reshape(row_blocks, tile_rows, 2 * NB)
    top_rows, diag_full = (
        lax.all_gather(factor_tops, "row", axis=1, tiled=True),
        lax.all_gather(diag_part, "row", axis=1, tiled=True),
    )
    top_rows = top_rows.reshape(2 * NB, local_cols)
    diag_full = diag_full.reshape(2 * NB, 2 * NB)
    owned_global = global_rows[:owned_rows]
    block_ids = jnp.arange(NB, dtype=jnp.int32)
    panel_globals = global_cols[split_col:]
    first_row = NB
    bottom = first_row + NB
    first_col = left_cols + first_row
    beneath = (global_rows >= bottom)[:, None]
    col_left = (global_cols < first_col)[None, :]
    adjoint_local = working[:, split_col:].reshape(local_rows, panel_cycles, tile_cols)
    adjoint_panels = lax.all_gather(adjoint_local, "col", axis=2, tiled=True).reshape(
        local_rows, 2 * NB
    )
    diag_block = diag_full[first_row:bottom, first_row:bottom]
    panel_factor = jnp.where(beneath, factor_panels[:, first_row:bottom], 0.0)
    solved_cols = lax.linalg.triangular_solve(
        diag_block, adjoint_panels[:, first_row:bottom], left_side=False, lower=True
    )
    column_adjoint = jnp.where(beneath, solved_cols, 0.0)
    picker = (owned_global[None, :] == first_row + block_ids[:, None]).astype(jnp.float32)
    partial_sum = exact_dot(picker, adjoint_panels[:owned_rows, first_row:bottom]) - jnp.tril(
        exact_dot(column_adjoint.T, panel_factor)
    )
    diag_start = lax.psum(partial_sum, "row")
    product = lower_half(exact_dot(diag_block.T, diag_start))
    left_solved = lax.linalg.triangular_solve(
        diag_block, product, left_side=True, lower=True, transpose_a=True
    )
    symmetric = lax.linalg.triangular_solve(diag_block, left_solved, left_side=False, lower=True)
    diag_adjoint = lower_half(symmetric + symmetric.T)
    owned_sym = exact_dot(picker.T, diag_adjoint + diag_adjoint.T)
    panel_rows_l = top_rows[first_row:bottom]
    trail_update = exact_dot(column_adjoint, panel_rows_l)
    row_extra = exact_dot(owned_sym, panel_rows_l)
    trail_factor = jnp.where(beneath & col_left, factor_flat, 0.0)
    row_terms = jnp.pad(
        exact_dot(column_adjoint.T, trail_factor), ((first_row, NB - first_row), (0, 0))
    ).reshape(row_blocks, row_span, local_cols)
    summed = lax.psum_scatter(row_terms, "row", scatter_dimension=1, tiled=True).reshape(
        owned_rows, local_cols
    )
    in_panel = ((owned_global >= first_row) & (owned_global < bottom))[:, None]
    row_change = jnp.where(in_panel & col_left, summed + row_extra, 0.0)
    working = working - jnp.where(beneath & col_left, trail_update, 0.0)
    working = jnp.concatenate([working[:owned_rows] - row_change, working[owned_rows:]], 0)
    owned_diag = exact_dot(picker.T, diag_adjoint)
    new_slot = jnp.where(beneath, column_adjoint, adjoint_panels[:, first_row:bottom])
    new_slot = jnp.concatenate(
        [jnp.where(in_panel, owned_diag, new_slot[:owned_rows]), new_slot[owned_rows:]], 0
    )
    new_panels = jnp.concatenate(
        [adjoint_panels[:, :first_row], new_slot, adjoint_panels[:, bottom:]], 1
    )
    local_new = lax.dynamic_index_in_dim(
        new_panels.reshape(local_rows, panel_cycles, col_devices, tile_cols),
        col_index,
        2,
        keepdims=False,
    ).reshape(local_rows, owned_cols)
    in_cols = ((panel_globals >= first_col) & (panel_globals < first_col + NB))[None, :]
    working = jnp.concatenate(
        [working[:, :split_col], jnp.where(in_cols, local_new, working[:, split_col:])], 1
    )
    return working.reshape(row_cycles, tile_rows, col_cycles, tile_cols)


def solution(mesh):
    in_specs = (P(None, "row", None, "col"), P(None, "row", None, "col"))
    out_specs = P(None, "row", None, "col")
    return jax.shard_map(local, mesh=mesh, in_specs=in_specs, out_specs=out_specs, check_vma=False)
```

profile of v0, /device:TPU:0, one launch (start us, length us, event | category | flops | bytes accessed | tf_op | source)
XLA Modules:
  0.0 376.3 jit_solution(3976893358861151109)
XLA Ops:
  6.5 2.7 copy.19
  9.4 1.2 copy-done.4
  10.7 1.4 copy.35
  12.2 40.3 %all-gather.7.cloned.1.call-done = f32[1152,2,512]{0,2,1:T(8,128)} async-done(((f32[1152,2,128]{0,2,1:T(8,128)}), f32[1152,2,512]{0,2,1:T(8,128)}) %all-gather.7.cloned.1.call-update) | async-done | bytes 4718608 | tf_op jit(solution)/shard_map/all_gather | solution.py:46
  52.5 1.9 slice.166
  54.4 1.2 copy.17
  55.9 1.2 copy-done.3
  57.2 1.4 copy.34
  60.3 68.9 %all-gather.9.cloned.1.call-done = f32[1,1024,1024]{1,2,0:T(8,128)} async-done(((f32[1,128,1024]{1,2,0:T(8,128)}), f32[1,1024,1024]{1,2,0:T(8,128)}) %all-gather.9.cloned.1.call-update) | async-done | bytes 4194320 | tf_op jit(solution)/shard_map/all_gather | solution.py:53
  129.2 1.3 fusion.19
  130.5 8.9 %while.1 = (s32[]{:T(128)}, f32[512,512]{0,1:T(8,128)S(1)}, s32[4,2]{0,1:T(2,128)S(1)}, f32[4,128,128]{2,1,0:T(8,128)S(1)}, s32[]{:T(128)}) while((s32[]{:T(128)}, f32[512,512]{0,1:T(8,128)S(1)}, s32[4,2]{0,1:T(2,128)S(1)}, f32[4,128,128]{2,1,0:T(8,128)S(1)}, s32[]{:T(128)}) %tuple.22), condition=%wide.while_cond, body=%wide.while_body.sunk | while | flops 2 | bytes 393329 | solution.py:71
  131.2 1.4 dynamic-slice.7
  133.4 1.4 dynamic-slice.7
  135.6 1.4 dynamic-slice.7
  137.8 1.4 dynamic-slice.7
  139.4 39.8 %custom-call.7 = f32[4,128,128]{1,2,0:T(8,128)S(1)} custom-call(f32[4,128,128]{2,1,0:T(8,128)S(1)} %get-tuple-element.12), custom_call_target="InvertDiagBlocksLowerTriangular" | custom-call | tf_op jit(solution)/shard_map/triangular_solve | solution.py:71
  179.3 1.9 fusion.34
  181.2 1.7 convolution_subtract_fusion.2
  183.6 2.0 convolution_subtract_fusion.1
  186.2 2.5 convolution_subtract_fusion
  188.7 1.5 fusion.69
  190.2 4.4 %fusion.9 = f32[512,512]{0,1:T(8,128)S(1)} fusion(f32[1152,1024]{0,1:T(8,128)S(1)} %bitcast.101, pred[1152]{0:T(1024)(128)(4,1)S(1)} %broadcast_compare_fusion, f32[1152,128]{0,1:T(8,128)S(1)} %fusion.34, f32[1152,128]{0,1:T(8,128)S(1)} %fusion.63, f32[1152,128]{0,1:T(8,128)S(1)} %fusion.66, f32[1152,128]{0,1:T(8,128)S(1)} %fusion.69), kind=kOutput, calls=%fused_computation.29 | convolution fusion | flops 3627352064 | bytes 5771264 | tf_op jit(solution)/shard_map/dot_general | solution.py:10
  194.6 2.7 convolution_subtract_fusion.3
  197.6 4.4 %fusion.102 = (f32[1152,512]{0,1:T(8,128)}, f32[1152,512]{0,1:T(8,128)S(1)}) fusion(f32[1152,1024]{0,1:T(8,128)} %bitcast.86, f32[1152,128]{0,1:T(8,128)S(1)} %fusion.34, f32[1152,128]{0,1:T(8,128)S(1)} %fusion.63, f32[1152,128]{0,1:T(8,128)S(1)} %fusion.66, f32[1152,128]{0,1:T(8,128)S(1)} %fusion.69, pred[1152]{0:T(1024)(128)(4,1)S(1)} %broadcast_compare_fusion), kind=kLoop, calls=%fused_computation.162 | loop fusion | flops 2949120 | bytes 11797632 | tf_op jit(solution)/shard_map/slice | solution.py:107
  202.0 1.5 copy-done.1
  203.5 1.6 slice.177
  205.1 7.7 %all-gather.11.cloned.1.call-done = f32[1,1024,384]{1,2,0:T(8,128)} async-done(((f32[1,128,384]{1,2,0:T(8,128)}), f32[1,1024,384]{1,2,0:T(8,128)}) %all-gather.11.cloned.1.call-update) | async-done | bytes 1572880 | tf_op jit(solution)/shard_map/all_gather | solution.py:52
  212.8 9.6 %fusion = f32[1152,384]{1,0:T(8,128)S(1)} fusion(f32[1152,384]{1,0:T(8,128)} %copy-done.3, pred[384]{0:T(512)(128)(4,1)S(1)} %broadcast_compare_fusion.1, pred[1152]{0:T(1024)(128)(4,1)S(1)} %broadcast_compare_fusion, f32[1,1024,384]{1,2,0:T(8,128)} %all-gather.11.cloned.1.call-done, f32[1152,128]{0,1:T(8,128)S(1)} %fusion.34, f32[1152,128]{0,1:T(8,128)S(1)} %fusion.63, ...), kind=kOutput, calls=%fused_computation.6 | convolution fusion | flops 2721595392 | bytes 6689280 | tf_op jit(solution)/shard_map/dot_general | solution.py:10
  222.4 1.2 slice.173
  223.6 1.4 copy-done.5
  225.1 4.7 %fusion.2 = f32[512,384]{1,0:T(8,128)S(1)} fusion(f32[1152,384]{1,0:T(8,128)S(1)} %bitcast.91, pred[384]{0:T(512)(128)(4,1)S(1)} %broadcast_compare_fusion.1, pred[1152]{0:T(1024)(128)(4,1)S(1)} %broadcast_compare_fusion, f32[1152,128]{0,1:T(8,128)S(1)} %fusion.34, f32[1152,128]{0,1:T(8,128)S(1)} %fusion.63, f32[1152,128]{0,1:T(8,128)S(1)} %fusion.66, ...), kind=kOutput, calls=%fused_computation.15 | convolution fusion | flops 2721153024 | bytes 4916736 | tf_op jit(solution)/shard_map/dot_general | solution.py:10
  229.8 1.3 pad_bitcast_fusion
  231.1 61.6 %all-reduce.3.cloned.1.call-done = f32[512,512]{0,1:T(8,128)} async-done(((f32[512,512]{0,1:T(8,128)}), f32[512,512]{0,1:T(8,128)}) %all-reduce.3.cloned.1.call-update) | async-done | bytes 1048592 | tf_op jit(solution)/shard_map/psum | solution.py:79
  292.7 3.4 convolution_bitcast_fusion
  296.1 4.5 %gather_fusion = f32[512]{0:T(512)S(1)} fusion(f32[512,512]{0,1:T(8,128)S(1)} %convolution_bitcast_fusion, s32[512]{0:T(512)S(1)} %bitcast.79), kind=kCustom, calls=%fused_computation | custom fusion | bytes 8192 | tf_op jit(solution)/shard_map/jit(_diag)/jit(diagonal)/cond/branch_0_fun/gather | solution.py:16
  303.6 1.5 convolution_subtract_fusion.9
  310.2 1.5 convolution_subtract_fusion.8
  312.1 1.1 pad_maximum_fusion.2
  314.7 4.8 %gather_fusion.1 = f32[512]{0:T(512)S(1)} fusion(f32[512,512]{0,1:T(8,128)S(1)} %bitcast_add_fusion.2, s32[512]{0:T(512)S(1)} %bitcast.80), kind=kCustom, calls=%fused_computation.1 | custom fusion | bytes 8192 | tf_op jit(solution)/shard_map/jit(_diag)/jit(diagonal)/cond/branch_0_fun/gather | solution.py:16
  319.6 1.3 copy.28
  321.0 1.6 convolution_select_fusion.1
  322.6 1.9 maximum_maximum_fusion
  325.0 2.1 fusion.18
  327.1 34.3 %reduce-scatter.2.cloned.1.call-done = f32[1,128,384]{2,1,0:T(8,128)} async-done(((f32[1,1024,384]{2,1,0:T(8,128)}), f32[1,128,384]{2,1,0:T(8,128)}) %reduce-scatter.2.cloned.1.call-update) | async-done | bytes 196624 | tf_op jit(solution)/shard_map/reduce_scatter | solution.py:94
  361.5 2.1 fusion.17
  363.7 1.3 fusion.3
  365.1 2.7 reshape.150
  367.7 1.4 copy.31
  (107 shorter events, 17.4 us)
Async XLA Ops:
  6.5 45.9 %all-gather.7.cloned.1.call-start = ((), (), s32[]{:S(2)}) async-start(), calls=%async_computation.2 | async-start | bytes 5898240 | tf_op jit(solution)/shard_map/all_gather | solution.py:46
  9.4 1.2 copy-start.4
  10.7 43.7 %copy-start.12 = (f32[9,128,3,128]{3,1,2,0:T(8,128)S(1)}, f32[9,128,3,128]{3,1,2,0:T(8,128)}, u32[]{:S(2)}) copy-start(f32[9,128,3,128]{3,1,2,0:T(8,128)} %param.3) | copy-start | bytes 5308420
  12.1 117.0 %all-gather.9.cloned.1.call-start = ((), (), s32[]{:S(2)}) async-start(), calls=%async_computation.3 | async-start | bytes 4718592 | tf_op jit(solution)/shard_map/all_gather | solution.py:53
  54.3 124.9 %all-gather.5.cloned.1.call-start = ((), (), s32[]{:S(2)}) async-start(), calls=%async_computation.1 | async-start | bytes 5898240 | tf_op jit(solution)/shard_map/all_gather | solution.py:66
  55.9 1.2 copy-start.3
  57.2 1.5 slice-start
  58.7 154.1 %all-gather.11.cloned.1.call-start = ((), (), s32[]{:S(2)}) async-start(), calls=%async_computation.4 | async-start | bytes 1769472 | tf_op jit(solution)/shard_map/all_gather | solution.py:52
  59.6 233.2 %all-reduce.3.cloned.1.call-start = ((), (), s32[]{:S(2)}) async-start(), calls=%async_computation.6 | async-start | bytes 2097152 | tf_op jit(solution)/shard_map/psum | solution.py:79
  59.6 164.0 %copy-start.13 = (pred[384]{0:T(512)(128)(4,1)}, pred[384]{0:T(512)(128)(4,1)S(1)}, u32[]{:S(2)}) copy-start(pred[384]{0:T(512)(128)(4,1)S(1)} %broadcast_compare_fusion.1) | copy-start | bytes 1156
  179.2 6.3 %copy-start.6 = (f32[4,128,128]{1,2,0:T(8,128)}, f32[4,128,128]{1,2,0:T(8,128)S(1)}, u32[]{:S(2)}) copy-start(f32[4,128,128]{1,2,0:T(8,128)S(1)} %custom-call.7) | copy-start | bytes 786436
  179.3 10.9 %slice-start.1 = ((s8[4718592]{0:T(1024)(128)(4,1)}), s8[4194304]{0:T(1024)(128)(4,1)S(1)}, s32[]{:S(2)}) async-start(s8[4718592]{0:T(1024)(128)(4,1)} %bitcast.99), calls=%async_computation.8 | async-start | bytes 8388608
  183.6 6.7 %slice-start.2 = ((s8[4718592]{0:T(1024)(128)(4,1)}), s8[524288]{0:T(1024)(128)(4,1)S(1)}, s32[]{:S(2)}) async-start(s8[4718592]{0:T(1024)(128)(4,1)} %bitcast.99), calls=%async_computation.9 | async-start | bytes 1048576
  197.4 164.1 %reduce-scatter.2.cloned.1.call-start = ((), (), s32[]{:S(2)}) async-start(), calls=%async_computation.5 | async-start | bytes 1769472 | tf_op jit(solution)/shard_map/reduce_scatter | solution.py:94
  202.0 1.5 copy-start.1
  222.4 7.5 %copy-start.11 = (f32[1152,384]{1,0:T(8,128)}, f32[1152,384]{1,0:T(8,128)S(1)}, u32[]{:S(2)}) copy-start(f32[1152,384]{1,0:T(8,128)S(1)} %fusion) | copy-start | bytes 5308420
  222.4 2.7 copy-start.5
  296.1 4.7 %copy-start.7 = (f32[4,128,128]{1,2,0:T(8,128)S(1)}, f32[4,128,128]{1,2,0:T(8,128)}, u32[]{:S(2)}) copy-start(f32[4,128,128]{1,2,0:T(8,128)} %copy-done.6) | copy-start | bytes 786436
  306.1 6.0 %copy-start.8 = (f32[512,128]{1,0:T(8,128)}, f32[512,128]{1,0:T(8,128)S(1)}, u32[]{:S(2)}) copy-start(f32[512,128]{1,0:T(8,128)S(1)} %copy.26) | copy-start | bytes 786436
  311.7 1.9 copy-start.9
  311.7 1.9 copy-start.10
  319.6 3.0 copy-start.2
  324.6 36.9 %copy-start.14 = (pred[384]{0:T(512)(128)(4,1)S(1)}, pred[384]{0:T(512)(128)(4,1)}, u32[]{:S(2)}) copy-start(pred[384]{0:T(512)(128)(4,1)} %copy-done.13) | copy-start | bytes 1156
  325.0 38.6 %copy-start.15 = (pred[256]{0:T(512)(128)(4,1)S(1)}, pred[256]{0:T(512)(128)(4,1)}, u32[]{:S(2)}) copy-start(pred[256]{0:T(512)(128)(4,1)} %compare_and_fusion) | copy-start | bytes 772
  327.1 36.5 %copy-start = (f32[1024,384]{1,0:T(8,128)S(1)}, f32[1024,384]{1,0:T(8,128)}, u32[]{:S(2)}) copy-start(f32[1024,384]{1,0:T(8,128)} %slice.173) | copy-start | bytes 4718596
Sparse Core Ops, SparseCore 0:
  12.3 40.1 all-gather.6
  54.5 74.6 all-gather.8
  130.7 35.6 all-gather.4
  168.3 44.4 all-gather.10
  216.2 76.5 all-reduce.2
  296.0 65.4 reduce-scatter.1
where the time goes:
time: 382 us; the launch traced here: 376 us
  waiting for transfers between devices  213 us (56%)
  other arithmetic  52.4 us (14%)
  matrix products  50.7 us (13%)
  local copies, waits for them, and re-layouts  45.4 us (12%)
  between operations  14.5 us (4%)
    all_gather x1, waiting for transfers between devices, local(): lax.all_gather(diag_part, 'row', axis=1, tiled=True)  68.9 us
    psum x1, waiting for transfers between devices, local(): diag_start = lax.psum(partial_sum, 'row')  61.6 us
    another operation x3, other arithmetic, local(): lax.linalg.triangular_solve(diag_block, adjoint_panels[:, first_row:botto...  41.2 us
    all_gather x1, waiting for transfers between devices, local(): lax.all_gather(factor_local, 'col', axis=2, tiled=True)  40.3 us
    reduce_scatter x1, waiting for transfers between devices, local(): lax.psum_scatter(row_terms, 'row', scatter_dimension=1, tiled=True)  34.3 us
    dot_general x8, matrix products, exact_dot(): jnp.dot(first, second, precision=lax.Precision.HIGHEST, preferred_element...  30.7 us
    another operation x7, matrix products, local(): lax.linalg.triangular_solve(diag_block, adjoint_panels[:, first_row:botto...  10.8 us
    unnamed x40, local copies, waits for them, and re-layouts  10.3 us
  transfers between devices with their start and end apart: 6, of which 5 were waited for; matrix products, arithmetic and copies ran while one was open for 34% of the time, Pallas kernels for 0%

commit v1 on v0

--- a/solution.py
+++ b/solution.py
@@ -4,6 +4,11 @@
 from jax.sharding import PartitionSpec as P
 
 NB = 512
+
+
+def all_parts(x, name, along):
+    pieces = lax.all_gather(x, name)
+    return jnp.concatenate(pieces, axis=along)
 
 
 def exact_dot(first, second):
@@ -50,7 +55,7 @@
     diag_part = factor_panels[:owned_rows].reshape(row_blocks, tile_rows, 2 * NB)
     top_rows, diag_full = (
         lax.all_gather(factor_tops, "row", axis=1, tiled=True),
-        lax.all_gather(diag_part, "row", axis=1, tiled=True),
+        all_parts(diag_part, "row", 1),
     )
     top_rows = top_rows.reshape(2 * NB, local_cols)
     diag_full = diag_full.reshape(2 * NB, 2 * NB)

time: 382 us -> 381 us (level)
    unnamed x40 -> x30, local copies, waits for them, and re-layouts: 10.3 us -> 10.9 us
    another operation x20 -> x13, local copies, waits for them, and re-layouts: 8.75 us -> 9.28 us
  transfers between devices with their start and end apart: 6 -> 6, of which waited for: 5 -> 5; matrix products, arithmetic and copies ran while one was open for 34% -> 33% of each run, Pallas kernels for 0% -> 0%
where the time goes in v1:
time: 381 us; the launch traced here: 375 us
  waiting for transfers between devices  216 us (57%)
  other arithmetic  50.8 us (13%)
  matrix products  49.2 us (13%)
  local copies, waits for them, and re-layouts  43.9 us (12%)
  between operations  14.4 us (4%)
    all_gather x1, waiting for transfers between devices, all_parts(): pieces = lax.all_gather(x, name)  67.6 us
    psum x1, waiting for transfers between devices, local(): diag_start = lax.psum(partial_sum, 'row')  61.5 us
    another operation x3, other arithmetic, local(): lax.linalg.triangular_solve(diag_block, adjoint_panels[:, first_row:botto...  41.2 us
    all_gather x1, waiting for transfers between devices, local(): lax.all_gather(factor_local, 'col', axis=2, tiled=True)  40.3 us
    reduce_scatter x1, waiting for transfers between devices, local(): lax.psum_scatter(row_terms, 'row', scatter_dimension=1, tiled=True)  37.8 us
    dot_general x8, matrix products, exact_dot(): jnp.dot(first, second, precision=lax.Precision.HIGHEST, preferred_element...  30.7 us
    unnamed x30, local copies, waits for them, and re-layouts  10.9 us
    another operation x7, matrix products, local(): lax.linalg.triangular_solve(diag_block, adjoint_panels[:, first_row:botto...  10.9 us
  transfers between devices with their start and end apart: 6, of which 5 were waited for; matrix products, arithmetic and copies ran while one was open for 33% of the time, Pallas kernels for 0%

profile of v1, /device:TPU:0, one launch (start us, length us, event | category | flops | bytes accessed | tf_op | source)
XLA Modules:
  0.0 374.8 jit_solution(15651831652108530650)
XLA Ops:
  6.5 2.7 copy.53
  9.4 1.2 copy-done.4
  10.7 1.4 copy.72
  12.2 40.3 %all-gather.7.cloned.1.call-done = f32[1152,2,512]{0,2,1:T(8,128)} async-done(((f32[1152,2,128]{0,2,1:T(8,128)}), f32[1152,2,512]{0,2,1:T(8,128)}) %all-gather.7.cloned.1.call-update) | async-done | bytes 4718608 | tf_op jit(solution)/shard_map/all_gather | solution.py:51
  52.4 1.1 slice.166
  53.5 1.0 copy.73
  54.6 1.2 copy.51
  56.1 1.2 copy-done.3
  57.4 1.4 copy.71
  59.9 67.6 %all-gather.9.cloned.1.call-done = f32[8,1,128,1024]{3,2,1,0:T(8,128)} async-done(((f32[1,1,128,1024]{3,2,1,0:T(8,128)}), f32[8,1,128,1024]{3,2,1,0:T(8,128)}) %all-gather.9.cloned.1.call-update) | async-done | bytes 4194320 | tf_op jit(solution)/shard_map/all_gather | solution.py:10
  127.5 1.4 fusion.19
  128.9 8.4 %while.1 = (s32[]{:T(128)}, f32[512,512]{1,0:T(8,128)S(1)}, s32[4,2]{0,1:T(2,128)S(1)}, f32[4,128,128]{2,1,0:T(8,128)S(1)}, s32[]{:T(128)}) while((s32[]{:T(128)}, f32[512,512]{1,0:T(8,128)S(1)}, s32[4,2]{0,1:T(2,128)S(1)}, f32[4,128,128]{2,1,0:T(8,128)S(1)}, s32[]{:T(128)}) %tuple.22), condition=%wide.while_cond, body=%wide.while_body.sunk | while | flops 2 | bytes 131189 | solution.py:76
  129.5 1.4 bitcast_dynamic-update-slice_fusion.2
  131.6 1.4 bitcast_dynamic-update-slice_fusion.2
  133.7 1.4 bitcast_dynamic-update-slice_fusion.2
  135.8 1.4 bitcast_dynamic-update-slice_fusion.2
  137.2 39.8 %custom-call.7 = f32[4,128,128]{1,2,0:T(8,128)S(1)} custom-call(f32[4,128,128]{2,1,0:T(8,128)S(1)} %get-tuple-element.12), custom_call_target="InvertDiagBlocksLowerTriangular" | custom-call | tf_op jit(solution)/shard_map/triangular_solve | solution.py:76
  177.1 1.9 fusion.34
  179.0 1.7 convolution_subtract_fusion.2
  181.4 2.0 convolution_subtract_fusion.1
  184.1 2.5 convolution_subtract_fusion
  186.6 1.5 fusion.70
  188.1 4.4 %fusion.9 = f32[512,512]{1,0:T(8,128)S(1)} fusion(f32[1152,1024]{0,1:T(8,128)S(1)} %bitcast.101, pred[1152]{0:T(1024)(128)(4,1)S(1)} %broadcast_compare_fusion, f32[1152,128]{0,1:T(8,128)S(1)} %fusion.34, f32[1152,128]{0,1:T(8,128)S(1)} %fusion.64, f32[1152,128]{0,1:T(8,128)S(1)} %fusion.67, f32[1152,128]{0,1:T(8,128)S(1)} %fusion.70), kind=kOutput, calls=%fused_computation.29 | convolution fusion | flops 3627352064 | bytes 5771264 | tf_op jit(solution)/shard_map/dot_general | solution.py:15
  192.5 2.6 convolution_subtract_fusion.3
  195.3 4.3 %fusion.103 = (f32[1152,512]{0,1:T(8,128)}, f32[1152,512]{0,1:T(8,128)S(1)}) fusion(f32[1152,1024]{0,1:T(8,128)} %bitcast.86, f32[1152,128]{0,1:T(8,128)S(1)} %fusion.34, f32[1152,128]{0,1:T(8,128)S(1)} %fusion.64, f32[1152,128]{0,1:T(8,128)S(1)} %fusion.67, f32[1152,128]{0,1:T(8,128)S(1)} %fusion.70, pred[1152]{0:T(1024)(128)(4,1)S(1)} %broadcast_compare_fusion), kind=kLoop, calls=%fused_computation.162 | loop fusion | flops 2949120 | bytes 11797632 | tf_op jit(solution)/shard_map/slice | solution.py:112
  199.6 1.5 copy-done.1
  201.1 1.6 slice.177
  202.7 8.9 %all-gather.11.cloned.1.call-done = f32[1,1024,384]{1,2,0:T(8,128)} async-done(((f32[1,128,384]{1,2,0:T(8,128)}), f32[1,1024,384]{1,2,0:T(8,128)}) %all-gather.11.cloned.1.call-update) | async-done | bytes 1572880 | tf_op jit(solution)/shard_map/all_gather | solution.py:57
  211.7 9.6 %fusion = f32[1152,384]{1,0:T(8,128)S(1)} fusion(f32[1152,384]{1,0:T(8,128)} %copy-done.3, pred[384]{0:T(512)(128)(4,1)S(1)} %broadcast_compare_fusion.1, pred[1152]{0:T(1024)(128)(4,1)S(1)} %broadcast_compare_fusion, f32[1,1024,384]{1,2,0:T(8,128)} %all-gather.11.cloned.1.call-done, f32[1152,128]{0,1:T(8,128)S(1)} %fusion.34, f32[1152,128]{0,1:T(8,128)S(1)} %fusion.64, ...), kind=kOutput, calls=%fused_computation.6 | convolution fusion | flops 2721595392 | bytes 6689280 | tf_op jit(solution)/shard_map/dot_general | solution.py:15
  221.3 1.2 slice.173
  222.5 1.4 copy-done.5
  223.9 4.7 %fusion.2 = f32[512,384]{1,0:T(8,128)S(1)} fusion(f32[1152,384]{1,0:T(8,128)S(1)} %bitcast.91, pred[384]{0:T(512)(128)(4,1)S(1)} %broadcast_compare_fusion.1, pred[1152]{0:T(1024)(128)(4,1)S(1)} %broadcast_compare_fusion, f32[1152,128]{0,1:T(8,128)S(1)} %fusion.34, f32[1152,128]{0,1:T(8,128)S(1)} %fusion.64, f32[1152,128]{0,1:T(8,128)S(1)} %fusion.67, ...), kind=kOutput, calls=%fused_computation.15 | convolution fusion | flops 2721153024 | bytes 4916736 | tf_op jit(solution)/shard_map/dot_general | solution.py:15
  228.7 1.2 pad_bitcast_fusion
  230.0 61.5 %all-reduce.3.cloned.1.call-done = f32[512,512]{1,0:T(8,128)} async-done(((f32[512,512]{1,0:T(8,128)}), f32[512,512]{1,0:T(8,128)}) %all-reduce.3.cloned.1.call-update) | async-done | bytes 1048592 | tf_op jit(solution)/shard_map/psum | solution.py:84
  291.5 3.4 convolution_bitcast_fusion
  294.9 4.5 %gather_fusion = f32[512]{0:T(512)S(1)} fusion(f32[512,512]{1,0:T(8,128)S(1)} %convolution_bitcast_fusion, s32[512]{0:T(512)S(1)} %bitcast.79), kind=kCustom, calls=%fused_computation | custom fusion | bytes 8192 | tf_op jit(solution)/shard_map/jit(_diag)/jit(diagonal)/cond/branch_0_fun/gather | solution.py:21
  305.6 1.5 convolution_subtract_fusion.8
  308.5 1.2 bitcast_add_fusion.2
  309.7 4.8 %gather_fusion.1 = f32[512]{0:T(512)S(1)} fusion(f32[512,512]{1,0:T(8,128)S(1)} %bitcast_add_fusion.2, s32[512]{0:T(512)S(1)} %bitcast.80), kind=kCustom, calls=%fused_computation.1 | custom fusion | bytes 8192 | tf_op jit(solution)/shard_map/jit(_diag)/jit(diagonal)/cond/branch_0_fun/gather | solution.py:21
  314.7 1.3 copy.62
  316.0 2.0 convolution_select_fusion.1
  318.1 1.9 maximum_maximum_fusion
  320.4 1.8 fusion.18
  322.3 37.8 %reduce-scatter.2.cloned.1.call-done = f32[1,128,384]{2,1,0:T(8,128)} async-done(((f32[1,1024,384]{2,1,0:T(8,128)}), f32[1,128,384]{2,1,0:T(8,128)}) %reduce-scatter.2.cloned.1.call-update) | async-done | bytes 196624 | tf_op jit(solution)/shard_map/reduce_scatter | solution.py:99
  360.1 2.1 fusion.17
  362.3 1.3 fusion.3
  363.6 2.7 reshape.142
  366.3 1.4 copy.65
  (87 shorter events, 14.2 us)
Async XLA Ops:
  6.5 45.9 %all-gather.7.cloned.1.call-start = ((), (), s32[]{:S(2)}) async-start(), calls=%async_computation.2 | async-start | bytes 5898240 | tf_op jit(solution)/shard_map/all_gather | solution.py:51
  9.4 1.2 copy-start.4
  12.1 42.5 %copy-start.10 = (f32[9,128,3,128]{3,1,2,0:T(8,128)S(1)}, f32[9,128,3,128]{3,1,2,0:T(8,128)}, u32[]{:S(2)}) copy-start(f32[9,128,3,128]{3,1,2,0:T(8,128)} %param.3) | copy-start | bytes 5308420
  12.1 115.4 %all-gather.9.cloned.1.call-start = ((), (), s32[]{:S(2)}) async-start(), calls=%async_computation.3 | async-start | bytes 4718592 | tf_op jit(solution)/shard_map/all_gather | solution.py:10
  54.5 122.5 %all-gather.5.cloned.1.call-start = ((), (), s32[]{:S(2)}) async-start(), calls=%async_computation.1 | async-start | bytes 5898240 | tf_op jit(solution)/shard_map/all_gather | solution.py:71
  56.1 1.2 copy-start.3
  57.4 1.5 slice-start
  58.9 152.8 %all-gather.11.cloned.1.call-start = ((), (), s32[]{:S(2)}) async-start(), calls=%async_computation.4 | async-start | bytes 1769472 | tf_op jit(solution)/shard_map/all_gather | solution.py:57
  59.8 231.7 %all-reduce.3.cloned.1.call-start = ((), (), s32[]{:S(2)}) async-start(), calls=%async_computation.6 | async-start | bytes 2097152 | tf_op jit(solution)/shard_map/psum | solution.py:84
  177.1 6.3 %copy-start.6 = (f32[4,128,128]{1,2,0:T(8,128)}, f32[4,128,128]{1,2,0:T(8,128)S(1)}, u32[]{:S(2)}) copy-start(f32[4,128,128]{1,2,0:T(8,128)S(1)} %custom-call.7) | copy-start | bytes 786436
  177.1 11.0 %slice-start.1 = ((s8[4718592]{0:T(1024)(128)(4,1)}), s8[4194304]{0:T(1024)(128)(4,1)S(1)}, s32[]{:S(2)}) async-start(s8[4718592]{0:T(1024)(128)(4,1)} %bitcast.99), calls=%async_computation.8 | async-start | bytes 8388608
  181.4 6.7 %slice-start.2 = ((s8[4718592]{0:T(1024)(128)(4,1)}), s8[524288]{0:T(1024)(128)(4,1)S(1)}, s32[]{:S(2)}) async-start(s8[4718592]{0:T(1024)(128)(4,1)} %bitcast.99), calls=%async_computation.9 | async-start | bytes 1048576
  195.1 164.9 %reduce-scatter.2.cloned.1.call-start = ((), (), s32[]{:S(2)}) async-start(), calls=%async_computation.5 | async-start | bytes 1769472 | tf_op jit(solution)/shard_map/reduce_scatter | solution.py:99
  199.6 1.5 copy-start.1
  221.2 7.4 %copy-start.9 = (f32[1152,384]{1,0:T(8,128)}, f32[1152,384]{1,0:T(8,128)S(1)}, u32[]{:S(2)}) copy-start(f32[1152,384]{1,0:T(8,128)S(1)} %fusion) | copy-start | bytes 5308420
  221.3 2.7 copy-start.5
  294.9 4.7 %copy-start.7 = (f32[4,128,128]{1,2,0:T(8,128)S(1)}, f32[4,128,128]{1,2,0:T(8,128)}, u32[]{:S(2)}) copy-start(f32[4,128,128]{1,2,0:T(8,128)} %copy-done.6) | copy-start | bytes 786436
  307.4 0.7 copy-start.8
  314.7 3.4 copy-start.2
  322.3 39.9 %copy-start = (f32[1024,384]{1,0:T(8,128)S(1)}, f32[1024,384]{1,0:T(8,128)}, u32[]{:S(2)}) copy-start(f32[1024,384]{1,0:T(8,128)} %slice.173) | copy-start | bytes 4718596
Sparse Core Ops, SparseCore 0:
  12.2 40.1 all-gather.6
  54.7 72.7 all-gather.8
  129.1 36.0 all-gather.4
  167.1 44.5 all-gather.10
  215.0 76.4 all-reduce.2
  294.8 65.2 reduce-scatter.1
